TPU v7x, 128 devices: a whole 4x4x4 slice. The times are simulated.
128 devices in a mesh: dp: 1, ep: 64 (over z, y, x), tp: 2 (over core).
Axes of the slice: x: 4, y: 4, z: 4, core: 2. Of those that a mesh axis runs over, the one named last changes fastest.
Arguments:
- x_in: bfloat16 [65536, 896], P(('dp', 'ep'))
- expert_ids: int32 [65536, 8], P(('dp', 'ep'))
- gate_vals: float32 [65536, 8], P(('dp', 'ep'))
- w_gate: bfloat16 [64, 896, 2560], P('ep', None, 'tp')
- w_up: bfloat16 [64, 896, 2560], P('ep', None, 'tp')
- w_down: bfloat16 [64, 2560, 896], P('ep', 'tp')
Outputs:
- output: bfloat16 [65536, 896], P(('dp', 'ep'))
All inputs are finite; a program needn't handle non-finite values.
Results may differ from a plain program's by a relative error of at most 0.0107107.
Values are sent between devices in bfloat16 or wider.
A program may use at most 1 GiB of HBM per device.

v0:
```python
import jax
import jax.numpy as jnp
from jax import lax
from jax.sharding import PartitionSpec as P

CAP_NUM = 5
CAP_DEN = 4


def local_routing(expert_ids, n_experts, capacity):
    tokens, n_top = expert_ids.shape
    flat_ids = expert_ids.reshape(tokens * n_top)
    onehot = (flat_ids[:, None] == jnp.arange(n_experts, dtype=jnp.int32)[None, :]).astype(jnp.int32)
    slots = jnp.sum((jnp.cumsum(onehot, axis=0) - onehot) * onehot, axis=1)
    flat_slot = jnp.where(slots < capacity, flat_ids * capacity + slots, n_experts * capacity)
    token_num = jnp.broadcast_to(jnp.arange(tokens, dtype=jnp.int32)[:, None], (tokens, n_top)).reshape(tokens * n_top)
    slot_owner = jnp.full((n_experts * capacity + 1,), tokens, jnp.int32).at[flat_slot].set(token_num)
    return slot_owner[: n_experts * capacity].reshape(n_experts, capacity), flat_slot.reshape(tokens, n_top)


def solution(mesh):
    n_ep = mesh.shape['ep']
    n_tp = mesh.shape['tp']
    row_spec = P(('dp', 'ep'), None)

    def device_body(x_loc, ids_loc, gates_loc, wg_loc, wu_loc, wd_loc):
        tokens, d_model = x_loc.shape
        n_top = ids_loc.shape[1]
        local_experts = wg_loc.shape[0]
        n_experts = local_experts * n_ep
        capacity = CAP_NUM * n_top * tokens // (CAP_DEN * n_experts)
        slot_share = capacity // n_tp
        slot_owner, flat_slot = local_routing(ids_loc, n_experts, capacity)
        my_owner = lax.dynamic_slice_in_dim(slot_owner, lax.axis_index('tp') * slot_share, slot_share, axis=1)
        outgoing = jnp.take(x_loc, my_owner, axis=0, mode='fill', fill_value=0)
        outgoing = outgoing.reshape(n_ep, local_experts, slot_share, d_model)
        arrived = lax.all_to_all(outgoing, 'ep', 0, 2, tiled=True).reshape(local_experts, n_ep * slot_share, d_model)
        gathered = lax.all_gather(arrived, 'tp', axis=1, tiled=True)
        h_gate = jnp.einsum('erd,edf->erf', gathered, wg_loc, preferred_element_type=jnp.float32)
        h_up = jnp.einsum('erd,edf->erf', gathered, wu_loc, preferred_element_type=jnp.float32)
        hidden = (jax.nn.silu(h_gate) * h_up).astype(jnp.bfloat16)
        part_out = jnp.einsum('erf,efd->erd', hidden, wd_loc, preferred_element_type=jnp.float32).astype(jnp.bfloat16)
        part_out = part_out.reshape(local_experts, n_tp, n_ep * slot_share, d_model)
        pieces = lax.all_to_all(part_out, 'tp', 1, 1, tiled=True)
        y_mine = jnp.sum(pieces, axis=1, dtype=jnp.float32).astype(jnp.bfloat16)
        returned = lax.all_to_all(y_mine.reshape(local_experts, n_ep, slot_share, d_model), 'ep', 1, 0, tiled=True)
        returned = returned.reshape(n_experts, slot_share, d_model)
        y_all = lax.all_gather(returned, 'tp', axis=1, tiled=True).reshape(n_experts * capacity, d_model)
        picked = jnp.take(y_all, flat_slot, axis=0, mode='fill', fill_value=0)
        return jnp.sum(picked * gates_loc[:, :, None], axis=1).astype(jnp.bfloat16)

    return jax.shard_map(device_body, mesh=mesh,
                         in_specs=(row_spec, row_spec, row_spec, P('ep', None, 'tp'), P('ep', None, 'tp'), P('ep', 'tp', None)),
                         out_specs=row_spec, check_vma=False)
```

profile of v0, /device:TPU:1, one launch (start us, length us, event | category | flops | bytes accessed | tf_op | source)
XLA Modules:
  0.0 697.4 jit_solution(914687343573295032)
XLA Ops:
  6.5 1.1 copy.13
  8.2 1.6 fusion.12
  9.8 36.3 %reduce-window.6 = s32[64,64,128]{2,1,0:T(8,128)} reduce-window(s32[64,64,128]{2,1,0:T(8,128)} %fusion.12, s32[]{:T(128)} %constant.25.clone.1), window={size=1x1x128 pad=0_0x0_0x127_0}, to_apply=%region_0.0 | reduce-window | flops 66584576 | bytes 4194308 | tf_op jit(solution)/shard_map/reduce-window
  46.2 3.3 slice_reduce_fusion
  49.7 2.9 broadcast_add_fusion
  52.6 0.3 mul.39
  53.2 3.5 fusion.11
  56.7 0.6 copy-done.4
  57.3 30.5 %scatter_custom_fusion = s32[10241]{0:T(1024)S(1)} fusion(s32[8192]{0:T(1024)S(1)} %bitcast.66, s32[8192]{0:T(1024)S(1)} %reshape.163, s32[]{:T(128)} %constant.30.clone.1), kind=kCustom, calls=%fused_computation.30 | custom fusion | bytes 40968 | tf_op jit(solution)/shard_map/scatter | solution.py:17
  88.1 26.3 %gather_fusion = bf16[5120,896]{1,0:T(8,128)(2,1)} fusion(bf16[1024,896]{1,0:T(8,128)(2,1)} %param.6, s32[5120]{0:T(1024)S(1)} %broadcast_clamp_fusion.1), kind=kCustom, calls=%fused_computation | custom fusion | bytes 18370560 | tf_op jit(solution)/shard_map/jit(_take)/gather | solution.py:35
  114.4 5.6 broadcast_select_fusion
  120.0 136.2 %all_to_all.23 = bf16[64,1,80,896]{3,2,1,0:T(8,128)(2,1)} all-to-all(bf16[64,1,80,896]{3,2,1,0:T(8,128)(2,1)S(1)} %broadcast_select_fusion), channel_id=1, replica_groups=mesh['dp'=1,'ep'=64,'tp'=2] {'ep'}, dimensions={0} | all-to-all | bytes 18350080 | tf_op jit(solution)/shard_map/all_to_all | solution.py:37
  256.4 39.1 %all-gather.4.cloned.1.call-done = bf16[1,10240,896]{2,1,0:T(8,128)(2,1)} async-done(((bf16[1,5120,896]{2,1,0:T(8,128)(2,1)}), bf16[1,10240,896]{2,1,0:T(8,128)(2,1)}) %all-gather.4.cloned.1.call-update) | async-done | bytes 18350096 | tf_op jit(solution)/shard_map/all_gather | solution.py:38
  295.5 35.0 %fusion.1 = f32[10240,1280]{1,0:T(8,128)} fusion(bf16[1,10240,896]{2,1,0:T(8,128)(2,1)} %all-gather.4.cloned.1.call-done, bf16[1,896,1280]{2,1,0:T(8,128)(2,1)S(1)} %copy-done), kind=kOutput, calls=%fused_computation.6 | convolution fusion | flops 23488102400 | bytes 73072640 | tf_op jit(solution)/shard_map/erd,edf->erf/dot_general | solution.py:39
  330.5 42.0 %multiply_convert_fusion.clone.4 = bf16[10240,1280]{1,0:T(8,128)(2,1)} fusion(f32[10240,1280]{1,0:T(8,128)} %fusion.1, bf16[1,10240,896]{2,1,0:T(8,128)(2,1)} %all-gather.4.cloned.1.call-done, bf16[1,896,1280]{2,1,0:T(8,128)(2,1)} %param.10), kind=kOutput, calls=%fused_computation.3.clone.clone.clone.1 | convolution fusion | flops 23566745600 | bytes 99287040 | tf_op jit(solution)/shard_map/erd,edf->erf/dot_general | solution.py:40
  372.4 34.1 %convolution_convert_fusion = bf16[10240,896]{1,0:T(8,128)(2,1)} fusion(bf16[1,1280,896]{2,1,0:T(8,128)(2,1)S(1)} %copy-done.7, bf16[10240,1280]{1,0:T(8,128)(2,1)} %multiply_convert_fusion.clone.4), kind=kOutput, calls=%fused_computation.8 | convolution fusion | flops 23497277440 | bytes 46858240 | tf_op jit(solution)/shard_map/erf,efd->erd/dot_general | solution.py:42
  406.5 33.8 %all_to_all.24 = bf16[1,2,5120,896]{3,2,0,1:T(8,128)(2,1)} all-to-all(bf16[1,2,5120,896]{3,2,0,1:T(8,128)(2,1)} %bitcast.62), channel_id=1, replica_groups=mesh['dp'=1,'ep'=64,'tp'=2] {'tp'}, dimensions={1} | all-to-all | bytes 36700160 | tf_op jit(solution)/shard_map/all_to_all | solution.py:44
  440.3 16.1 %reduce_sum.37 = bf16[5120,896]{1,0:T(8,128)(2,1)} reduce(bf16[1,2,5120,896]{3,2,0,1:T(8,128)(2,1)} %all_to_all.24, bf16[]{:T(256)} %constant.52.clone.1), dimensions={0,1}, to_apply=%region_4.5 | reduce | flops 4587520 | bytes 27525122 | tf_op jit(solution)/shard_map/reduce_sum | solution.py:45
  456.4 132.1 %all_to_all.25 = bf16[1,64,80,896]{3,2,0,1:T(8,128)(2,1)} all-to-all(bf16[1,64,80,896]{3,2,0,1:T(8,128)(2,1)} %bitcast.60), channel_id=1, replica_groups=mesh['dp'=1,'ep'=64,'tp'=2] {'ep'}, dimensions={1} | all-to-all | bytes 18350080 | tf_op jit(solution)/shard_map/all_to_all | solution.py:46
  588.6 0.7 copy-done.5
  589.4 0.3 reduce_sum.35
  590.4 34.9 %all-gather.6.cloned.1.call-done = bf16[1,64,160,896]{3,2,0,1:T(8,128)(2,1)} async-done(((bf16[1,64,80,896]{3,2,0,1:T(8,128)(2,1)}), bf16[1,64,160,896]{3,2,0,1:T(8,128)(2,1)}) %all-gather.6.cloned.1.call-update) | async-done | bytes 18350096 | tf_op jit(solution)/shard_map/all_gather | solution.py:48
  625.2 47.3 %gather_fusion.1 = bf16[8192,896]{1,0:T(8,128)(2,1)} fusion(bf16[10240,896]{1,0:T(8,128)(2,1)} %bitcast.58, s32[8192]{0:T(1024)S(1)} %broadcast_clamp_fusion), kind=kCustom, calls=%fused_computation.1 | custom fusion | bytes 29392896 | tf_op jit(solution)/shard_map/jit(_take)/gather | solution.py:49
  672.6 17.5 %multiply_reduce_fusion = bf16[1024,896]{1,0:T(8,128)(2,1)} fusion(bf16[8192,896]{1,0:T(8,128)(2,1)} %gather_fusion.1, f32[1024,8]{1,0:T(8,128)S(1)} %copy.18, pred[1024,8]{1,0:T(8,128)(4,1)S(1)} %get-tuple-element.5), kind=kLoop, calls=%fused_computation.4 | loop fusion | flops 28442624 | bytes 16556032 | tf_op jit(solution)/shard_map/reduce_sum | solution.py:50
  (34 shorter events, 2.3 us)
Async XLA Ops:
  6.5 289.0 %copy-start = (bf16[1,896,1280]{2,1,0:T(8,128)(2,1)S(1)}, bf16[1,896,1280]{2,1,0:T(8,128)(2,1)}, u32[]{:S(2)}) copy-start(bf16[1,896,1280]{2,1,0:T(8,128)(2,1)} %param.9) | copy-start | bytes 6881284
  6.5 289.0 %all-gather.4.cloned.1.call-start = ((), (), s32[]{:S(2)}) async-start(), calls=%async_computation.3 | async-start | bytes 27525120 | tf_op jit(solution)/shard_map/all_gather | solution.py:38
  7.6 49.0 %copy-start.2 = (s32[1024,8]{1,0:T(8,128)}, s32[1024,8]{1,0:T(8,128)S(1)}, u32[]{:S(2)}) copy-start(s32[1024,8]{1,0:T(8,128)S(1)} %copy.13) | copy-start | bytes 98308
  56.7 0.6 copy-start.4
  256.2 369.1 %all-gather.6.cloned.1.call-start = ((), (), s32[]{:S(2)}) async-start(), calls=%async_computation.4 | async-start | bytes 27525120 | tf_op jit(solution)/shard_map/all_gather | solution.py:48
  330.5 42.0 %copy-start.7 = (bf16[1,1280,896]{2,1,0:T(8,128)(2,1)S(1)}, bf16[1,1280,896]{2,1,0:T(8,128)(2,1)}, u32[]{:S(2)}) copy-start(bf16[1,1280,896]{2,1,0:T(8,128)(2,1)} %param.11) | copy-start | bytes 6881284
  588.6 0.8 copy-start.5
  588.6 1.1 copy-start.3
  588.6 1.5 copy-start.6
  625.2 64.9 %copy-start.1 = (bf16[1,896,1280]{2,1,0:T(8,128)(2,1)S(1)}, bf16[1,896,1280]{2,1,0:T(8,128)(2,1)}, u32[]{:S(2)}) copy-start(bf16[1,896,1280]{2,1,0:T(8,128)(2,1)} %param.9) | copy-start | bytes 6881284
Sparse Core Ops, SparseCore 0:
  256.3 39.1 all-gather.3
  588.7 36.4 all-gather.5
where the time goes:
time: 709 us; the launch traced here: 697 us
  blocking collectives  302 us (43%)
  local copies, waits for them, and re-layouts  112 us (16%)
  matrix products  111 us (16%)
  other arithmetic  84.2 us (12%)
  waiting for transfers between devices  74 us (10%)
  between operations  14 us (2%)
    all_to_all x1, blocking collectives, device_body(): lax.all_to_all(outgoing, 'ep', 0, 2, tiled=True)  136 us
    all_to_all x1, blocking collectives, device_body(): lax.all_to_all(y_mine.reshape(local_experts, n_ep, slot_share, d_model),...  132 us
    gather x1, local copies, waits for them, and re-layouts, device_body(): picked = jnp.take(y_all, flat_slot, axis=0, mode='fill', fill_value=0)  47.3 us
    dot_general x1, matrix products, device_body(): jnp.einsum('erd,edf->erf', gathered, wu_loc, preferred_element_type=jnp.f...  42 us
    another operation x3, other arithmetic  39.5 us
    all_gather x1, waiting for transfers between devices, device_body(): gathered = lax.all_gather(arrived, 'tp', axis=1, tiled=True)  39.1 us
    dot_general x1, matrix products, device_body(): jnp.einsum('erd,edf->erf', gathered, wg_loc, preferred_element_type=jnp.f...  35 us
    all_gather x1, waiting for transfers between devices, device_body(): lax.all_gather(returned, 'tp', axis=1, tiled=True)  34.9 us
  transfers between devices with their start and end apart: 2, of which 2 were waited for; matrix products, arithmetic and copies ran while one was open for 0% of the time, Pallas kernels for 0%

commit v1 on v0

v1 whole, which is shorter than its diff:
```python
import functools

import jax
import jax.numpy as jnp
from jax import lax
from jax.experimental import pallas as pl
from jax.experimental.pallas import tpu as pltpu
from jax.sharding import PartitionSpec as P

MESH = pl.DeviceIdType.MESH
CAP_NUM = 5
CAP_DEN = 4
GROUP = 4
LEAD = 4
LAG = 6
STEP = 37
F_BLOCK = 512


def moe_kernel(x_ref, ids_ref, gates_ref, wg_hbm, wu_hbm, wd_hbm, o_ref,
               src, arr, ret, wg, wu, wd, pos, g1, g2, g3, onehot, hid, wt, y3, acc, other,
               w_sem, ws_sem, wr_sem, ds_sem, dr_sem, bs_sem, br_sem, xs_sem, xr_sem):
    core = lax.axis_index('tp')
    me = lax.axis_index('ep')
    cx, cy, cz = lax.rem(me, 4), lax.rem(me // 4, 4), me // 16
    tokens, d_model = x_ref.shape
    n_top = ids_ref.shape[0]
    n_groups, rows, _ = src.shape
    share = rows // GROUP
    n_exp = n_groups * GROUP
    half = wg_hbm.shape[2]
    bf16, f32 = jnp.bfloat16, jnp.float32

    def partner(k, sign):
        d = lax.rem(STEP * k, n_exp)
        dx, dy, dz = lax.rem(d, 4), lax.rem(d // 4, 4), d // 16
        if sign < 0:
            dx, dy, dz = 4 - dx, 4 - dy, 4 - dz
        return lax.rem(cx + dx, 4) + 4 * lax.rem(cy + dy, 4) + 16 * lax.rem(cz + dz, 4)

    own = pl.ds(pl.multiple_of(core * half, 128), half)
    spots = ((wg_hbm, wg.at[:, own]), (wu_hbm, wu.at[:, own]), (wd_hbm, wd.at[own, :]))
    local_w, remote_w = [], []
    for i, (hbm, dst) in enumerate(spots):
        local_w.append(pltpu.make_async_copy(hbm.at[0], dst, w_sem.at[i]))
        remote_w.append(pltpu.make_async_remote_copy(
            src_ref=hbm.at[0], dst_ref=dst, send_sem=ws_sem.at[i], recv_sem=wr_sem.at[i],
            device_id={'tp': 1 - core}, device_id_type=MESH))
    for c in local_w + remote_w:
        c.start()

    exp_iota = lax.broadcasted_iota(jnp.int32, (n_exp, 128), 0)
    tri = (lax.broadcasted_iota(jnp.int32, (128, 128), 0)
           < lax.broadcasted_iota(jnp.int32, (128, 128), 1)).astype(f32).astype(bf16)
    before = jnp.zeros((n_exp, 1), f32)
    for b in range(tokens // 128):
        cols = pl.ds(b * 128, 128)
        hot = jnp.zeros((n_exp, 128), f32)
        gate = jnp.zeros((n_exp, 128), f32)
        for j in range(n_top):
            hit = exp_iota == ids_ref[j:j + 1, cols]
            hot = jnp.where(hit, 1.0, hot)
            gate = jnp.where(hit, gates_ref[j:j + 1, cols], gate)
        count = jnp.dot(hot.astype(bf16), tri, preferred_element_type=f32) + before
        pos[:, cols] = jnp.where(hot > 0.0, count, -1.0)
        before = before + jnp.sum(hot, axis=1, keepdims=True)
        p1 = gate.astype(bf16).astype(f32)
        p2 = (gate - p1).astype(bf16).astype(f32)
        g1[:, cols] = p1
        g2[:, cols] = p2
        g3[:, cols] = gate - p1 - p2

    slot_iota = (lax.broadcasted_iota(jnp.int32, (share, tokens), 0) + core * share).astype(f32)

    def send_out(k):
        return pltpu.make_async_remote_copy(
            src_ref=src.at[k // GROUP, pl.ds(pl.multiple_of(lax.rem(k, GROUP) * share, 16), share)],
            dst_ref=arr.at[k // GROUP, pl.ds(pl.multiple_of(lax.rem(k, GROUP) * share, 16), share)],
            send_sem=ds_sem.at[k], recv_sem=dr_sem.at[k],
            device_id={'ep': partner(k, 1)}, device_id_type=MESH)

    def send_back(k):
        return pltpu.make_async_remote_copy(
            src_ref=arr.at[k // GROUP, pl.ds(pl.multiple_of(lax.rem(k, GROUP) * share, 16), share)],
            dst_ref=ret.at[k // GROUP, pl.ds(pl.multiple_of(lax.rem(k, GROUP) * share, 16), share)],
            send_sem=bs_sem.at[k], recv_sem=br_sem.at[k],
            device_id={'ep': partner(k, -1)}, device_id_type=MESH)

    def each(g, fn):
        def one(i, carry):
            k = g * GROUP + i

            @pl.when(k > 0)
            def _():
                fn(k)
            return carry
        lax.fori_loop(0, GROUP, one, 0)

    def dispatch(g):
        for i in range(GROUP):
            row = pos[pl.ds(partner(g * GROUP + i, 1), 1), :]
            onehot[pl.ds(i * share, share), :] = jnp.where(row == slot_iota, 1.0, 0.0).astype(bf16)
        src[g] = jnp.dot(onehot[...], x_ref[...], preferred_element_type=f32).astype(bf16)

        @pl.when(g == 0)
        def _():
            arr[0, 0:share, :] = src[0, 0:share, :]
        each(g, lambda k: send_out(k).start())

    def experts(g):
        each(g, lambda k: send_out(k).wait_recv())

        def block(f, carry):
            cols = pl.ds(pl.multiple_of(f * F_BLOCK, F_BLOCK), F_BLOCK)
            a = jnp.dot(arr[g], wg[:, cols], preferred_element_type=f32)
            b = jnp.dot(arr[g], wu[:, cols], preferred_element_type=f32)
            hid[:, cols] = (a * jax.nn.sigmoid(a) * b).astype(bf16)
            return carry
        lax.fori_loop(0, 2 * half // F_BLOCK, block, 0)
        arr[g] = jnp.dot(hid[...], wd[...], preferred_element_type=f32).astype(bf16)

        @pl.when(g == 0)
        def _():
            ret[0, 0:share, :] = arr[0, 0:share, :]
        each(g, lambda k: send_back(k).start())

    def combine(g, after=None):
        each(g, lambda k: send_back(k).wait_recv())
        for i in range(GROUP):
            e = pl.ds(partner(g * GROUP + i, 1), 1)
            hit = pos[e, :] == slot_iota
            for p, part in enumerate((g1, g2, g3)):
                wt[pl.ds(p * rows + i * share, share), :] = jnp.where(hit, part[e, :], 0.0).astype(bf16)
        for p in range(3):
            y3[pl.ds(p * rows, rows), :] = ret[g]
        for b in range(2):
            blk = pl.ds(b * (tokens // 2), tokens // 2)
            acc[blk, :] += lax.dot_general(wt[:, blk], y3[...], (((0,), (0,)), ((), ())),
                                           preferred_element_type=f32)
            if after is not None:
                after(b)

    def swap(b):
        blk = pl.ds(b * (tokens // 2), tokens // 2)
        return pltpu.make_async_remote_copy(
            src_ref=acc.at[blk], dst_ref=other.at[blk], send_sem=xs_sem.at[b], recv_sem=xr_sem.at[b],
            device_id={'tp': 1 - core}, device_id_type=MESH)

    acc[...] = jnp.zeros_like(acc)

    def ahead(g, carry):
        dispatch(g)
        return carry
    lax.fori_loop(0, LEAD, ahead, 0)
    for c in local_w:
        c.wait()
    for c in remote_w:
        c.wait()

    def step(g, carry):
        @pl.when(g + LEAD < n_groups)
        def _():
            dispatch(g + LEAD)

        @pl.when(g < n_groups)
        def _():
            experts(g)

        @pl.when(g >= LAG)
        def _():
            combine(g - LAG)
        return carry
    lax.fori_loop(0, n_groups + LAG - 1, step, 0)
    combine(n_groups - 1, lambda b: swap(b).start())

    def drain(k, carry):
        send_out(k).wait_send()
        send_back(k).wait_send()
        return carry
    lax.fori_loop(1, n_exp, drain, 0)
    for b in range(2):
        blk = pl.ds(b * (tokens // 2), tokens // 2)
        swap(b).wait()
        o_ref[blk, :] = (acc[blk, :] + other[blk, :]).astype(bf16)


def solution(mesh):
    n_ep = mesh.shape['ep']
    n_tp = mesh.shape['tp']
    row_spec = P(('dp', 'ep'), None)
    vmem = pl.BlockSpec(memory_space=pltpu.VMEM)
    hbm = pl.BlockSpec(memory_space=pl.ANY)

    def device_body(x_loc, ids_loc, gates_loc, wg_loc, wu_loc, wd_loc):
        tokens, d_model = x_loc.shape
        n_top = ids_loc.shape[1]
        n_experts = wg_loc.shape[0] * n_ep
        width = wg_loc.shape[2] * n_tp
        capacity = CAP_NUM * n_top * tokens // (CAP_DEN * n_experts)
        share = capacity // n_tp
        rows, n_groups = GROUP * share, n_experts // GROUP
        bf16, f32 = jnp.bfloat16, jnp.float32
        scratch = [
            pltpu.VMEM((n_groups, rows, d_model), bf16),
            pltpu.VMEM((n_groups, rows, d_model), bf16),
            pltpu.VMEM((n_groups, rows, d_model), bf16),
            pltpu.VMEM((d_model, width), bf16),
            pltpu.VMEM((d_model, width), bf16),
            pltpu.VMEM((width, d_model), bf16),
            pltpu.VMEM((n_experts, tokens), f32),
            pltpu.VMEM((n_experts, tokens), f32),
            pltpu.VMEM((n_experts, tokens), f32),
            pltpu.VMEM((n_experts, tokens), f32),
            pltpu.VMEM((rows, tokens), bf16),
            pltpu.VMEM((rows, width), bf16),
            pltpu.VMEM((3 * rows, tokens), bf16),
            pltpu.VMEM((3 * rows, d_model), bf16),
            pltpu.VMEM((tokens, d_model), f32),
            pltpu.VMEM((tokens, d_model), f32),
            pltpu.SemaphoreType.DMA((3,)),
            pltpu.SemaphoreType.DMA((3,)),
            pltpu.SemaphoreType.DMA((3,)),
            pltpu.SemaphoreType.DMA((n_experts,)),
            pltpu.SemaphoreType.DMA((n_experts,)),
            pltpu.SemaphoreType.DMA((n_experts,)),
            pltpu.SemaphoreType.DMA((n_experts,)),
            pltpu.SemaphoreType.DMA((2,)),
            pltpu.SemaphoreType.DMA((2,)),
        ]
        return pl.pallas_call(
            moe_kernel,
            out_shape=jax.ShapeDtypeStruct((tokens, d_model), bf16),
            in_specs=[vmem, vmem, vmem, hbm, hbm, hbm],
            out_specs=vmem,
            scratch_shapes=scratch,
            compiler_params=pltpu.CompilerParams(has_side_effects=True, vmem_limit_bytes=67043328),
        )(x_loc, ids_loc.T, gates_loc.T, wg_loc, wu_loc, wd_loc)

    return jax.shard_map(device_body, mesh=mesh,
                         in_specs=(row_spec, row_spec, row_spec, P('ep', None, 'tp'), P('ep', None, 'tp'), P('ep', 'tp', None)),
                         out_specs=row_spec, check_vma=False)
```

time: 709 us -> 299 us (0.42)
  the two profiles are of different devices: /device:TPU:1 before, /device:TPU:7 now
where the time goes in v1:
time: 299 us
  Pallas kernels  296 us (99%)
    pallas_call x1, Pallas kernels, device_body(): pl.pallas_call(moe_kernel, out_shape=jax.ShapeDtypeStruct((tokens, d_mode...  296 us

profile of v1, /device:TPU:7, one launch (start us, length us, event | category | flops | bytes accessed | tf_op | source)
XLA Modules:
  0.0 299.2 jit_solution(194743668441324098)
XLA Ops:
  0.0 296.3 %shard_map.64 = bf16[1024,896]{1,0:T(8,128)(2,1)} custom-call(bf16[1024,896]{1,0:T(8,128)(2,1)} %x_ref.1, s32[8,1024]{1,0:T(8,128)} %bitcast.2, f32[8,1024]{1,0:T(8,128)} %bitcast.3, bf16[1,896,1280]{2,1,0:T(8,128)(2,1)} %wg_hbm.1, bf16[1,896,1280]{2,1,0:T(8,128)(2,1)} %wu_hbm.1, bf16[1,1280,896]{2,1,0:T(8,128)(2,1)} %wd_hbm.1), custom_call_target="tpu_custom_call" | custom-call | tf_op jit(solution)/shard_map/pallas_call | solution.py:230
  296.3 2.9 copy.8

commit v2 on v1

v2 whole, which is shorter than its diff:
```python
import functools

import jax
import jax.numpy as jnp
from jax import lax
from jax.experimental import pallas as pl
from jax.experimental.pallas import tpu as pltpu
from jax.sharding import PartitionSpec as P

MESH = pl.DeviceIdType.MESH
CAP_NUM = 5
CAP_DEN = 4
PARTS = (32, 32, 16)
LEAD = 6
LAGS = (0, 2, 4, 6, 8, 10)
SIDE = 4
F_BLOCK = 512


def moe_kernel(x_ref, ids_ref, gates_ref, wg_hbm, wu_hbm, wd_hbm, o_ref, r1, r2, r4, r5,
               src, arr, ret, wg, wu, wd, pos, g1, g2, g3, onehot, hid, wt, y3, acc, other,
               w_sem, ws_sem, wr_sem, p1s, p1r, q1s, q1r, p2s, p2r, p3s, p3r, q3s, q3r, q2s, q2r,
               out_sem, in_sem, xs_sem, xr_sem):
    core = lax.axis_index('tp')
    me = lax.axis_index('ep')
    here = (lax.rem(me, SIDE), lax.rem(me // SIDE, SIDE), me // (SIDE * SIDE))
    tokens, d_model = x_ref.shape
    n_top = ids_ref.shape[0]
    n_chunks, rows, _ = src.shape
    share = rows // SIDE
    n_exp = n_chunks * SIDE
    half = wg_hbm.shape[2]
    bf16, f32 = jnp.bfloat16, jnp.float32
    colors = range(len(PARTS))
    first = [SIDE * sum(PARTS[:r]) for r in colors]

    def device(r, d, sign):
        e = d if sign > 0 else tuple(SIDE - v for v in d)
        out = 0
        for axis, scale in ((0, 1), (1, SIDE), (2, SIDE * SIDE)):
            v0, v1 = e[(axis - r) % 3], e[(axis - r - 1) % 3]
            out = out + scale * lax.rem(here[axis] + v0 + core * (v1 - v0), SIDE)
        return out

    def offs(c):
        db = lax.rem(c, SIDE)
        return db, lax.rem(db + c // SIDE, SIDE)

    def piece(r, da):
        return pl.ds(first[r] + da * PARTS[r], PARTS[r])

    def block(r):
        return pl.ds(first[r], SIDE * PARTS[r])

    def remote(a, b, s_sem, r_sem, dev):
        return pltpu.make_async_remote_copy(src_ref=a, dst_ref=b, send_sem=s_sem, recv_sem=r_sem,
                                            device_id={'ep': dev}, device_id_type=MESH)

    def p1(r, c, da, dst):
        return remote(src.at[c, piece(r, da)], dst.at[c, piece(r, da)], p1s.at[r, c, da - 1], p1r.at[r, c, da - 1],
                      device(r, (da, 0, 0), 1))

    def p2(r, c, dst):
        return remote(r1.at[c, block(r)], dst.at[c, block(r)], p2s.at[r, c], p2r.at[r, c],
                      device(r, (0, offs(c)[0], 0), 1))

    def p3(r, c, a):
        return remote(a.at[c, block(r)], arr.at[c, block(r)], p3s.at[r, c], p3r.at[r, c],
                      device(r, (0, 0, offs(c)[1]), 1))

    def q3(r, c, dst):
        return remote(arr.at[c, block(r)], dst.at[c, block(r)], q3s.at[r, c], q3r.at[r, c],
                      device(r, (0, 0, offs(c)[1]), -1))

    def q2(r, c, a):
        return remote(a.at[c, block(r)], r5.at[c, block(r)], q2s.at[r, c], q2r.at[r, c],
                      device(r, (0, offs(c)[0], 0), -1))

    def q1(r, c, da, a):
        return remote(a.at[c, piece(r, da)], ret.at[c, piece(r, da)], q1s.at[r, c, da - 1], q1r.at[r, c, da - 1],
                      device(r, (da, 0, 0), -1))

    def own_out(r, c):
        return pltpu.make_async_copy(src.at[c, piece(r, 0)], r1.at[c, piece(r, 0)], out_sem.at[r, c])

    def own_in(r, c):
        return pltpu.make_async_copy(r5.at[c, piece(r, 0)], ret.at[c, piece(r, 0)], in_sem.at[r, c])

    own = pl.ds(pl.multiple_of(core * half, 128), half)
    spots = ((wg_hbm, wg.at[:, own]), (wu_hbm, wu.at[:, own]), (wd_hbm, wd.at[own, :]))
    local_w, remote_w = [], []
    for i, (hbm, dst) in enumerate(spots):
        local_w.append(pltpu.make_async_copy(hbm.at[0], dst, w_sem.at[i]))
        remote_w.append(pltpu.make_async_remote_copy(
            src_ref=hbm.at[0], dst_ref=dst, send_sem=ws_sem.at[i], recv_sem=wr_sem.at[i],
            device_id={'tp': 1 - core}, device_id_type=MESH))
    for c in local_w + remote_w:
        c.start()

    exp_iota = lax.broadcasted_iota(jnp.int32, (n_exp, 128), 0)
    tri = (lax.broadcasted_iota(jnp.int32, (128, 128), 0)
           < lax.broadcasted_iota(jnp.int32, (128, 128), 1)).astype(f32).astype(bf16)
    before = jnp.zeros((n_exp, 1), f32)
    for b in range(tokens // 128):
        cols = pl.ds(b * 128, 128)
        hot = jnp.zeros((n_exp, 128), f32)
        gate = jnp.zeros((n_exp, 128), f32)
        for j in range(n_top):
            hit = exp_iota == ids_ref[j:j + 1, cols]
            hot = jnp.where(hit, 1.0, hot)
            gate = jnp.where(hit, gates_ref[j:j + 1, cols], gate)
        count = jnp.dot(hot.astype(bf16), tri, preferred_element_type=f32) + before
        pos[:, cols] = jnp.where(hot > 0.0, count, -1.0)
        before = before + jnp.sum(hot, axis=1, keepdims=True)
        part1 = gate.astype(bf16).astype(f32)
        part2 = (gate - part1).astype(bf16).astype(f32)
        g1[:, cols] = part1
        g2[:, cols] = part2
        g3[:, cols] = gate - part1 - part2

    def slots(r):
        start = core * share + sum(PARTS[:r])
        return (lax.broadcasted_iota(jnp.int32, (PARTS[r], tokens), 0) + start).astype(f32)

    def send_out(c):
        db, dc = offs(c)
        for r in colors:
            want = slots(r)
            for da in range(SIDE):
                row = pos[pl.ds(device(r, (da, db, dc), 1), 1), :]
                onehot[piece(r, da), :] = jnp.where(row == want, 1.0, 0.0).astype(bf16)
        src[c] = jnp.dot(onehot[...], x_ref[...], preferred_element_type=f32).astype(bf16)

        @pl.when(c == 0)
        def _():
            for r in colors:
                arr[0, piece(r, 0), :] = src[0, piece(r, 0), :]
                for da in (2, 1, 3):
                    p1(r, c, da, arr).start()

        @pl.when(c > 0)
        def _():
            for r in colors:
                own_out(r, c).start()
                for da in (2, 1, 3):
                    p1(r, c, da, r1).start()

    def relay_b(c):
        db, dc = offs(c)

        @pl.when(c == 0)
        def _():
            for r in colors:
                for da in (1, 2, 3):
                    p1(r, c, da, arr).wait_recv()

        @pl.when(c > 0)
        def _():
            for r in colors:
                own_out(r, c).wait()
                for da in (1, 2, 3):
                    p1(r, c, da, r1).wait_recv()

        @pl.when((db > 0) & (dc == 0))
        def _():
            for r in colors:
                p2(r, c, arr).start()

        @pl.when((db > 0) & (dc > 0))
        def _():
            for r in colors:
                p2(r, c, r2).start()

        @pl.when((db == 0) & (dc > 0))
        def _():
            for r in colors:
                p3(r, c, r1).start()

    def relay_c(c):
        db, dc = offs(c)

        @pl.when((db > 0) & (dc > 0))
        def _():
            for r in colors:
                p2(r, c, r2).wait_recv()
                p3(r, c, r2).start()

    def experts(c):
        db, dc = offs(c)

        @pl.when((db > 0) & (dc == 0))
        def _():
            for r in colors:
                p2(r, c, arr).wait_recv()

        @pl.when(dc > 0)
        def _():
            for r in colors:
                p3(r, c, r2).wait_recv()

        def part(f, carry):
            cols = pl.ds(pl.multiple_of(f * F_BLOCK, F_BLOCK), F_BLOCK)
            a = jnp.dot(arr[c], wg[:, cols], preferred_element_type=f32)
            b = jnp.dot(arr[c], wu[:, cols], preferred_element_type=f32)
            hid[:, cols] = (a * jax.nn.sigmoid(a) * b).astype(bf16)
            return carry
        lax.fori_loop(0, 2 * half // F_BLOCK, part, 0)
        arr[c] = jnp.dot(hid[...], wd[...], preferred_element_type=f32).astype(bf16)

        @pl.when((db > 0) & (dc > 0))
        def _():
            for r in colors:
                q3(r, c, r4).start()

        @pl.when((db == 0) & (dc > 0))
        def _():
            for r in colors:
                q3(r, c, r5).start()

        @pl.when((db > 0) & (dc == 0))
        def _():
            for r in colors:
                q2(r, c, arr).start()

        @pl.when(c == 0)
        def _():
            for r in colors:
                ret[0, piece(r, 0), :] = arr[0, piece(r, 0), :]
                for da in (2, 1, 3):
                    q1(r, c, da, arr).start()

    def back_b(c):
        db, dc = offs(c)

        @pl.when((db > 0) & (dc > 0))
        def _():
            for r in colors:
                q3(r, c, r4).wait_recv()
                q2(r, c, r4).start()

    def back_a(c):
        db, dc = offs(c)

        @pl.when((db == 0) & (dc > 0))
        def _():
            for r in colors:
                q3(r, c, r5).wait_recv()

        @pl.when(db > 0)
        def _():
            for r in colors:
                q2(r, c, r4).wait_recv()

        @pl.when(c > 0)
        def _():
            for r in colors:
                own_in(r, c).start()
                for da in (2, 1, 3):
                    q1(r, c, da, r5).start()

    def combine(c, after=None):
        db, dc = offs(c)
        for r in colors:
            for da in (1, 2, 3):
                q1(r, c, da, r5).wait_recv()

        @pl.when(c > 0)
        def _():
            for r in colors:
                own_in(r, c).wait()
        for r in colors:
            want = slots(r)
            for da in range(SIDE):
                e = pl.ds(device(r, (da, db, dc), 1), 1)
                hit = pos[e, :] == want
                for p, part in enumerate((g1, g2, g3)):
                    wt[pl.ds(p * rows + first[r] + da * PARTS[r], PARTS[r]), :] = (
                        jnp.where(hit, part[e, :], 0.0).astype(bf16))
        for p in range(3):
            y3[pl.ds(p * rows, rows), :] = ret[c]
        for b in range(2):
            blk = pl.ds(b * (tokens // 2), tokens // 2)
            acc[blk, :] += lax.dot_general(wt[:, blk], y3[...], (((0,), (0,)), ((), ())),
                                           preferred_element_type=f32)
            if after is not None:
                after(b)

    def swap(b):
        blk = pl.ds(b * (tokens // 2), tokens // 2)
        return pltpu.make_async_remote_copy(
            src_ref=acc.at[blk], dst_ref=other.at[blk], send_sem=xs_sem.at[b], recv_sem=xr_sem.at[b],
            device_id={'tp': 1 - core}, device_id_type=MESH)

    acc[...] = jnp.zeros_like(acc)

    def ahead(c, carry):
        send_out(c)
        return carry
    lax.fori_loop(0, LEAD, ahead, 0)
    for c in local_w:
        c.wait()
    for c in remote_w:
        c.wait()

    def step(t, carry):
        def at(c, fn):
            @pl.when((c >= 0) & (c < n_chunks))
            def _():
                fn(c)
        at(t + LEAD, send_out)
        at(t - LAGS[4], back_a)
        at(t - LAGS[3], back_b)
        at(t - LAGS[1], relay_c)
        at(t - LAGS[0], relay_b)
        at(t - LAGS[2], experts)

        @pl.when((t >= LAGS[5]))
        def _():
            combine(t - LAGS[5])
        return carry
    lax.fori_loop(0, n_chunks + LAGS[5] - 1, step, 0)
    combine(n_chunks - 1, lambda b: swap(b).start())

    def drain(c, carry):
        db, dc = offs(c)
        for r in colors:
            for da in (1, 2, 3):
                p1(r, c, da, r1).wait_send()
                q1(r, c, da, r5).wait_send()

        @pl.when(db > 0)
        def _():
            for r in colors:
                p2(r, c, r2).wait_send()
                q2(r, c, r4).wait_send()

        @pl.when(dc > 0)
        def _():
            for r in colors:
                p3(r, c, r2).wait_send()
                q3(r, c, r4).wait_send()
        return carry
    lax.fori_loop(0, n_chunks, drain, 0)
    for b in range(2):
        blk = pl.ds(b * (tokens // 2), tokens // 2)
        swap(b).wait()
        o_ref[blk, :] = (acc[blk, :] + other[blk, :]).astype(bf16)


def solution(mesh):
    n_ep = mesh.shape['ep']
    n_tp = mesh.shape['tp']
    row_spec = P(('dp', 'ep'), None)
    vmem = pl.BlockSpec(memory_space=pltpu.VMEM)
    hbm = pl.BlockSpec(memory_space=pl.ANY)

    def device_body(x_loc, ids_loc, gates_loc, wg_loc, wu_loc, wd_loc):
        tokens, d_model = x_loc.shape
        n_top = ids_loc.shape[1]
        n_experts = wg_loc.shape[0] * n_ep
        width = wg_loc.shape[2] * n_tp
        capacity = CAP_NUM * n_top * tokens // (CAP_DEN * n_experts)
        share = capacity // n_tp
        rows, n_groups = SIDE * share, n_experts // SIDE
        bf16, f32 = jnp.bfloat16, jnp.float32
        scratch = [
            pltpu.VMEM((n_groups, rows, d_model), bf16),
            pltpu.VMEM((n_groups, rows, d_model), bf16),
            pltpu.VMEM((n_groups, rows, d_model), bf16),
            pltpu.VMEM((d_model, width), bf16),
            pltpu.VMEM((d_model, width), bf16),
            pltpu.VMEM((width, d_model), bf16),
            pltpu.VMEM((n_experts, tokens), f32),
            pltpu.VMEM((n_experts, tokens), f32),
            pltpu.VMEM((n_experts, tokens), f32),
            pltpu.VMEM((n_experts, tokens), f32),
            pltpu.VMEM((rows, tokens), bf16),
            pltpu.VMEM((rows, width), bf16),
            pltpu.VMEM((3 * rows, tokens), bf16),
            pltpu.VMEM((3 * rows, d_model), bf16),
            pltpu.VMEM((tokens, d_model), f32),
            pltpu.VMEM((tokens, d_model), f32),
            pltpu.SemaphoreType.DMA((3,)),
            pltpu.SemaphoreType.DMA((3,)),
            pltpu.SemaphoreType.DMA((3,)),
            pltpu.SemaphoreType.DMA((len(PARTS), n_groups, SIDE - 1)),
            pltpu.SemaphoreType.DMA((len(PARTS), n_groups, SIDE - 1)),
            pltpu.SemaphoreType.DMA((len(PARTS), n_groups, SIDE - 1)),
            pltpu.SemaphoreType.DMA((len(PARTS), n_groups, SIDE - 1)),
            pltpu.SemaphoreType.DMA((len(PARTS), n_groups)),
            pltpu.SemaphoreType.DMA((len(PARTS), n_groups)),
            pltpu.SemaphoreType.DMA((len(PARTS), n_groups)),
            pltpu.SemaphoreType.DMA((len(PARTS), n_groups)),
            pltpu.SemaphoreType.DMA((len(PARTS), n_groups)),
            pltpu.SemaphoreType.DMA((len(PARTS), n_groups)),
            pltpu.SemaphoreType.DMA((len(PARTS), n_groups)),
            pltpu.SemaphoreType.DMA((len(PARTS), n_groups)),
            pltpu.SemaphoreType.DMA((len(PARTS), n_groups)),
            pltpu.SemaphoreType.DMA((len(PARTS), n_groups)),
            pltpu.SemaphoreType.DMA((2,)),
            pltpu.SemaphoreType.DMA((2,)),
        ]
        return pl.pallas_call(
            moe_kernel,
            out_shape=[jax.ShapeDtypeStruct((tokens, d_model), bf16)]
            + [jax.ShapeDtypeStruct((n_groups, rows, d_model), bf16)] * 4,
            in_specs=[vmem, vmem, vmem, hbm, hbm, hbm],
            out_specs=[vmem, hbm, hbm, hbm, hbm],
            scratch_shapes=scratch,
            compiler_params=pltpu.CompilerParams(has_side_effects=True, vmem_limit_bytes=67043328),
        )(x_loc, ids_loc.T, gates_loc.T, wg_loc, wu_loc, wd_loc)[0]

    return jax.shard_map(device_body, mesh=mesh,
                         in_specs=(row_spec, row_spec, row_spec, P('ep', None, 'tp'), P('ep', None, 'tp'), P('ep', 'tp', None)),
                         out_specs=row_spec, check_vma=False)
```

time: 299 us -> 263 us (0.88)
  the two profiles are of different devices: /device:TPU:7 before, /device:TPU:1 now
where the time goes in v2:
time: 263 us; the launch traced here: 262 us
  Pallas kernels  260 us (99%)
  local copies, waits for them, and re-layouts  2.87 us (1%)
    pallas_call x1, Pallas kernels, device_body(): pl.pallas_call(moe_kernel, out_shape=[jax.ShapeDtypeStruct((tokens, d_mod...  260 us

profile of v2, /device:TPU:1, one launch (start us, length us, event | category | flops | bytes accessed | tf_op | source)
XLA Modules:
  0.0 262.4 jit_solution(686182375989575503)
XLA Ops:
  0.0 259.5 %shard_map.64 = (bf16[1024,896]{1,0:T(8,128)(2,1)}, bf16[16,320,896]{2,1,0:T(8,128)(2,1)}, bf16[16,320,896]{2,1,0:T(8,128)(2,1)}, bf16[16,320,896]{2,1,0:T(8,128)(2,1)}, bf16[16,320,896]{2,1,0:T(8,128)(2,1)}) custom-call(bf16[1024,896]{1,0:T(8,128)(2,1)} %x_ref.1, s32[8,1024]{1,0:T(8,128)} %bitcast.2, f32[8,1024]{1,0:T(8,128)} %bitcast.3, ...), custom_call_target="tpu_custom_call" | custom-call | tf_op jit(solution)/shard_map/pallas_call | solution.py:403
  259.5 2.9 %copy.8 = bf16[1024,896]{1,0:T(8,128)(2,1)} copy(bf16[1024,896]{1,0:T(8,128)(2,1)} %get-tuple-element.6) | data formatting | bytes 3670016
